TPU v7x, 32 devices: a whole 2x2x4 slice. The times are simulated.
32 devices in a mesh: wide: 2 (over x), narrow: 4 (over y, core), depth: 4 (over z).
Axes of the slice: x: 2, y: 2, z: 4, core: 2. Of those that a mesh axis runs over, the one named last changes fastest.
Arguments:
- patch_store: bfloat16 [8, 1024, 4096], P('wide', 'depth'), may hold values from -6 to 6
- w_key: bfloat16 [4096, 1024], P(None, 'narrow'), may hold values from -0.09375 to 0.09375
- w_value: bfloat16 [4096, 1024], P(None, 'narrow'), may hold values from -0.09375 to 0.09375
- key_gain: float32 [128], replicated, may hold values from 0.1 to 1.9
- query_gain: float32 [128], replicated, may hold values from 0.1 to 1.9
- queries: bfloat16 [32, 4096], P('wide', 'narrow'), may hold values from -6 to 6
- owner_table: int32 [8], replicated, may hold values from 0 to 7, each once
- reader_table: int32 [2, 2], replicated, may hold values from 0 to 7
- request_image: int32 [32], P('wide'), may hold values from 0 to 1
- image_tiles: int32 [8], replicated, may hold values from 1 to 4
Outputs:
- context: bfloat16 [32, 4096], P(('wide', 'depth'), 'narrow')
Inputs may be any that keep to these rules, and one draw needn't show every extreme that they name: owner_table is a permutation of the slots. `reader_table`: entries are image ids; a group's list may repeat an image.
All inputs are finite; a program needn't handle non-finite values.
Results may differ from a plain program's by a relative error of at most 0.012.
Values may be sent and summed in bfloat16 or wider, within the bound.
A program may use at most 64 MiB of HBM per device.

v0:
```python
import math
import jax
import jax.numpy as jnp
from jax import lax
from jax.sharding import PartitionSpec as P

HD = 128
TILE_P = 256
epsilon = 1e-05


def rms_scaled(tensor, scaling):
    return tensor / jnp.sqrt(jnp.mean(tensor * tensor, axis=-1, keepdims=True) + epsilon) * scaling


def local(
    patch_store,
    w_key,
    w_value,
    key_gain,
    query_gain,
    queries,
    owner_table,
    reader_table,
    request_image,
    image_tiles,
):
    images_here, rows_here, model_width = patch_store.shape
    kv_cols = w_key.shape[1]
    kv_local = kv_cols // HD
    patch_rows = patch_store.reshape(images_here * rows_here, model_width)
    key_rows = jnp.dot(patch_rows, w_key, preferred_element_type=jnp.float32).reshape(
        images_here, rows_here, kv_local, HD
    )
    key_rows = (
        rms_scaled(key_rows, key_gain)
        .astype(jnp.bfloat16)
        .reshape(images_here, rows_here * kv_cols)
    )
    values = jnp.dot(patch_rows, w_value, preferred_element_type=jnp.float32).astype(jnp.bfloat16)
    values = values.reshape(images_here, rows_here * kv_cols)
    owner_index = lax.axis_index("wide")
    wanted = owner_table[reader_table]
    read_count = reader_table.shape[1]
    batch_here = queries.shape[0]
    group_size = queries.shape[1] // (kv_local * HD)
    normed = rms_scaled(
        queries.astype(jnp.float32).reshape(batch_here, kv_local, group_size, HD), query_gain
    ).astype(jnp.bfloat16)
    row_ids = lax.axis_index("depth") * rows_here + jnp.arange(rows_here, dtype=jnp.int32)
    scale = 1.0 / math.sqrt(HD)
    local_slots = owner_index * images_here + jnp.arange(images_here, dtype=jnp.int32)
    picker = (wanted[:, :, None] == local_slots[None, None, :]).astype(jnp.bfloat16)
    send_keys = jnp.einsum(
        "wrj,jx->wrx", picker, key_rows, preferred_element_type=jnp.float32
    ).astype(jnp.bfloat16)
    send_values = jnp.einsum(
        "wrj,jx->wrx", picker, values, preferred_element_type=jnp.float32
    ).astype(jnp.bfloat16)
    got_keys, got_values = (
        lax.all_to_all(send_keys, "wide", split_axis=0, concat_axis=0, tiled=True),
        lax.all_to_all(send_values, "wide", split_axis=0, concat_axis=0, tiled=True),
    )
    read_keys = jnp.sum(got_keys, axis=0, dtype=jnp.float32).astype(jnp.bfloat16)
    read_values = jnp.sum(got_values, axis=0, dtype=jnp.float32).astype(jnp.bfloat16)
    read_keys = read_keys.reshape(read_count, rows_here, kv_local, HD)
    read_values = read_values.reshape(read_count, rows_here, kv_local, HD)
    scores = (
        jnp.einsum("bkgd,rskd->bkgrs", normed, read_keys, preferred_element_type=jnp.float32)
        * scale
    )
    my_images = reader_table[owner_index]
    chosen = (request_image[:, None] == jnp.arange(read_count, dtype=jnp.int32)[None, :]).astype(
        jnp.float32
    )
    usable = (row_ids[None, :] // TILE_P < image_tiles[my_images][:, None]).astype(jnp.float32)
    weights = jnp.exp(scores) * chosen[:, None, None, :, None] * usable[None, None, None]
    denominator = jnp.sum(weights, axis=(3, 4)).reshape(batch_here, kv_local * group_size)
    numerator = jnp.einsum(
        "bkgrs,rskd->bkgd",
        weights.astype(jnp.bfloat16),
        read_values,
        preferred_element_type=jnp.float32,
    )
    numerator = numerator.reshape(batch_here, kv_local * group_size * HD)
    row_share = batch_here // lax.axis_size("depth")
    numerator, denominator = (
        lax.psum(numerator.astype(jnp.bfloat16), "depth").astype(jnp.float32),
        lax.psum(denominator.astype(jnp.bfloat16), "depth").astype(jnp.float32),
    )
    first_row = lax.axis_index("depth") * row_share
    numerator = lax.dynamic_slice_in_dim(numerator, first_row, row_share, 0)
    denominator = lax.dynamic_slice_in_dim(denominator, first_row, row_share, 0)
    heads_here = denominator.shape[1]
    context = numerator.reshape(row_share, heads_here, HD) / denominator[:, :, None]
    return context.reshape(row_share, heads_here * HD).astype(jnp.bfloat16)


def solution(mesh):
    placed = (
        P("wide", "depth", None),
        P(None, "narrow"),
        P(None, "narrow"),
        P(),
        P(),
        P("wide", "narrow"),
        P(),
        P(),
        P("wide"),
        P(),
    )
    return jax.shard_map(
        local, mesh=mesh, in_specs=placed, out_specs=P(("wide", "depth"), "narrow"), check_vma=False
    )
```

profile of v0, /device:TPU:0, one launch (start us, length us, event | category | flops | bytes accessed | tf_op | source)
XLA Modules:
  0.0 63.2 jit_solution(15374107702283691047)
XLA Ops:
  0.0 4.3 %copy.48 = bf16[256,4096]{1,0:T(8,128)(2,1)} copy(bf16[256,4096]{0,1:T(8,128)(2,1)} %bitcast.51) | data formatting | bytes 4194304 | tf_op jit(solution)/shard_map/dot_general | solution.py:32
  4.3 6.4 %multiply_reduce_fusion = (f32[4,256,2]{1,2,0:T(2,128)S(1)}, f32[4,256,2,128]{1,3,2,0:T(8,128)S(1)}) fusion(bf16[2,128,4096,1]{2,1,0,3:T(8,128)(2,1)} %bitcast.52, bf16[4,256,4096]{2,1,0:T(8,128)(2,1)} %param.10), kind=kOutput, calls=%fused_computation.16 | convolution fusion | flops 2148005888 | bytes 11542528 | tf_op jit(solution)/shard_map/dot_general | solution.py:32
  10.7 0.1 multiply_convert_fusion
  10.8 0.4 copy.32
  11.3 0.2 reshape.199
  11.5 0.1 reshape.180
  11.6 0.6 %gather_fusion = s32[4]{0:T(128)S(1)} fusion(s32[8]{0:T(128)S(1)} %copy-done.1, s32[1024]{0:T(1024)S(1)} %pad_clamp_fusion.1), kind=kCustom, calls=%fused_computation | custom fusion | bytes 48 | tf_op jit(solution)/shard_map/gather | solution.py:43
  12.2 0.1 reshape.179
  12.3 1.4 %convolution_convert_fusion = bf16[2,2,65536]{2,1,0:T(2,128)(2,1)} fusion(bf16[4,65536,1]{1,0,2:T(4,128)(2,1)S(1)} %reshape.199, s32[4]{0:T(128)S(1)} %iota_add_fusion, s32[2,2]{1,0:T(2,128)S(1)} %reshape.179), kind=kOutput, calls=%fused_computation.2 | convolution fusion | flops 2359312 | bytes 1048608 | tf_op jit(solution)/shard_map/wrj,jx->wrx/dot_general | solution.py:54
  13.7 4.2 %all-to-all-start.1 = ((bf16[2,2,65536]{2,1,0:T(2,128)(2,1)}), bf16[2,2,65536]{2,1,0:T(2,128)(2,1)S(1)}, u32[]{:S(2)}, u32[]{:S(2)}) async-start(bf16[2,2,65536]{2,1,0:T(2,128)(2,1)} %convolution_convert_fusion), calls=%async_computation.1 | async-start | bytes 1048576 | tf_op jit(solution)/shard_map/all_to_all | solution.py:61
  18.0 0.1 multiply_reduce_fusion.1
  18.1 0.1 copy.33
  18.2 0.6 %gather_fusion.1 = s32[2]{0:T(128)S(1)} fusion(s32[8]{0:T(128)S(1)} %copy-done.2, s32[1024]{0:T(1024)S(1)} %pad_clamp_fusion), kind=kCustom, calls=%fused_computation.1 | custom fusion | bytes 24 | tf_op jit(solution)/shard_map/gather | solution.py:76
  18.9 6.5 %convolution_convert_fusion.2 = bf16[1024,256]{1,0:T(8,128)(2,1)} fusion(bf16[1024,4096]{1,0:T(8,128)(2,1)} %bitcast.56, bf16[4096,256]{1,0:T(8,128)(2,1)S(1)} %copy-done), kind=kOutput, calls=%fused_computation.6 | convolution fusion | flops 2147745792 | bytes 11010048 | tf_op jit(solution)/shard_map/dot_general | solution.py:40
  25.4 0.1 compare_convert_fusion
  25.5 1.4 %reshape.196 = bf16[4,65536,1]{1,0,2:T(4,128)(2,1)S(1)} reshape(bf16[1024,256]{1,0:T(8,128)(2,1)} %convolution_convert_fusion.2) | data formatting | bytes 1048576 | tf_op jit(solution)/shard_map/reshape | solution.py:41
  26.9 1.4 %convolution_convert_fusion.1 = bf16[2,2,65536]{2,1,0:T(2,128)(2,1)} fusion(bf16[4,65536,1]{1,0,2:T(4,128)(2,1)S(1)} %reshape.196, s32[4]{0:T(128)S(1)} %iota_add_fusion, s32[2,2]{1,0:T(2,128)S(1)} %reshape.179), kind=kOutput, calls=%fused_computation.3 | convolution fusion | flops 2359312 | bytes 1048608 | tf_op jit(solution)/shard_map/wrj,jx->wrx/dot_general | solution.py:57
  28.3 3.5 %all-to-all-start = ((bf16[2,2,65536]{2,1,0:T(2,128)(2,1)}), bf16[2,2,65536]{2,1,0:T(2,128)(2,1)S(1)}, u32[]{:S(2)}, u32[]{:S(2)}) async-start(bf16[2,2,65536]{2,1,0:T(2,128)(2,1)} %convolution_convert_fusion.1), calls=%async_computation | async-start | bytes 1048576 | tf_op jit(solution)/shard_map/all_to_all | solution.py:62
  31.8 0.1 copy.34
  31.9 0.1 fusion.12
  32.0 1.1 %reduce_sum.53 = bf16[2,65536]{1,0:T(2,128)(2,1)S(1)} reduce(bf16[2,2,65536]{2,1,0:T(2,128)(2,1)S(1)} %all-to-all-done.1, bf16[]{:T(256)} %constant.16.clone.1), dimensions={0}, to_apply=%region_2.0 | reduce | flops 131072 | bytes 786434 | tf_op jit(solution)/shard_map/reduce_sum | solution.py:64
  33.2 0.2 reshape.173
  33.4 7.1 %all-to-all-done = bf16[2,2,65536]{2,1,0:T(2,128)(2,1)S(1)} async-done(((bf16[2,2,65536]{2,1,0:T(2,128)(2,1)}), bf16[2,2,65536]{2,1,0:T(2,128)(2,1)S(1)}, u32[]{:S(2)}, u32[]{:S(2)}) %all-to-all-start) | async-done | bytes 524320 | tf_op jit(solution)/shard_map/all_to_all | solution.py:62
  40.5 1.1 %reduce_sum.51 = bf16[2,65536]{1,0:T(2,128)(2,1)S(1)} reduce(bf16[2,2,65536]{2,1,0:T(2,128)(2,1)S(1)} %all-to-all-done, bf16[]{:T(256)} %constant.16.clone.1), dimensions={0}, to_apply=%region_0.0 | reduce | flops 131072 | bytes 786434 | tf_op jit(solution)/shard_map/reduce_sum | solution.py:65
  41.7 0.2 reshape.171
  41.9 0.3 fusion.22
  42.2 0.2 fusion.7
  42.4 19.9 %all-reduce = (bf16[16,8]{0,1:T(8,128)(2,1)S(1)}, bf16[16,1024]{1,0:T(8,128)(2,1)S(1)}) all-reduce(bf16[16,8]{0,1:T(8,128)(2,1)S(1)} %bitcast.55, bf16[16,1024]{1,0:T(8,128)(2,1)S(1)} %convert_element_type.72), channel_id=1, replica_groups=mesh['wide'=2,'narrow'=4,'depth'=4] {'depth'}, use_global_device_ids=true, to_apply=%region_6.7 | all-reduce | flops 16512 | bytes 66048 | tf_op jit(solution)/shard_map/psum | solution.py:89
  62.3 0.1 constant_dynamic-slice_fusion
  62.4 0.1 copy.40
  62.5 0.1 broadcast_bitcast_fusion
  62.6 0.6 fusion.13
  (30 shorter events, 0.2 us)
Async XLA Ops:
  0.0 18.9 %copy-start = (bf16[4096,256]{1,0:T(8,128)(2,1)S(1)}, bf16[4096,256]{1,0:T(8,128)(2,1)}, u32[]{:S(2)}) copy-start(bf16[4096,256]{1,0:T(8,128)(2,1)} %param.12) | copy-start | bytes 6291460
  4.3 6.4 %copy-start.5 = (f32[128]{0:T(128)S(1)}, f32[128]{0:T(128)}, u32[]{:S(2)}) copy-start(f32[128]{0:T(128)} %param.13) | copy-start | bytes 1540
  10.6 0.8 %copy-start.4 = (s32[2,2]{1,0:T(2,128)S(1)}, s32[2,2]{1,0:T(2,128)}, u32[]{:S(2)}) copy-start(s32[2,2]{1,0:T(2,128)} %param.17) | copy-start | bytes 52
  10.7 0.9 %copy-start.1 = (s32[8]{0:T(128)S(1)}, s32[8]{0:T(128)}, u32[]{:S(2)}) copy-start(s32[8]{0:T(128)} %param.16) | copy-start | bytes 100
  11.3 6.7 %copy-start.3 = (bf16[16,1024]{1,0:T(8,128)(2,1)S(1)}, bf16[16,1024]{1,0:T(8,128)(2,1)}, u32[]{:S(2)}) copy-start(bf16[16,1024]{1,0:T(8,128)(2,1)} %param.15) | copy-start | bytes 98308
  11.3 7.0 %copy-start.2 = (s32[8]{0:T(128)S(1)}, s32[8]{0:T(128)}, u32[]{:S(2)}) copy-start(s32[8]{0:T(128)} %param.19) | copy-start | bytes 100
  13.7 14.6 %all-to-all-start.1 = ((bf16[2,2,65536]{2,1,0:T(2,128)(2,1)}), bf16[2,2,65536]{2,1,0:T(2,128)(2,1)S(1)}, u32[]{:S(2)}, u32[]{:S(2)}) async-start(bf16[2,2,65536]{2,1,0:T(2,128)(2,1)} %convolution_convert_fusion), calls=%async_computation.1 | async-start | bytes 1048576 | tf_op jit(solution)/shard_map/all_to_all | solution.py:61
  25.4 6.4 %copy-start.7 = (s32[16]{0:T(128)S(1)}, s32[16]{0:T(128)}, u32[]{:S(2)}) copy-start(s32[16]{0:T(128)} %param.18) | copy-start | bytes 196
  25.4 6.5 %copy-start.6 = (f32[128]{0:T(128)S(1)}, f32[128]{0:T(128)}, u32[]{:S(2)}) copy-start(f32[128]{0:T(128)} %param.14) | copy-start | bytes 1540
  28.3 12.2 %all-to-all-start = ((bf16[2,2,65536]{2,1,0:T(2,128)(2,1)}), bf16[2,2,65536]{2,1,0:T(2,128)(2,1)S(1)}, u32[]{:S(2)}, u32[]{:S(2)}) async-start(bf16[2,2,65536]{2,1,0:T(2,128)(2,1)} %convolution_convert_fusion.1), calls=%async_computation | async-start | bytes 1048576 | tf_op jit(solution)/shard_map/all_to_all | solution.py:62
where the time goes:
time: 63.5 us; the launch traced here: 63.2 us
  blocking collectives  19.9 us (31%)
  matrix products  16.1 us (25%)
  local copies, waits for them, and re-layouts  8.68 us (14%)
  starting transfers between devices  7.75 us (12%)
  waiting for transfers between devices  7.14 us (11%)
  other arithmetic  3.42 us (5%)
    psum x1, blocking collectives, local(): lax.psum(denominator.astype(jnp.bfloat16), 'depth').astype(jnp.float32)  19.9 us
    all_to_all x1, waiting for transfers between devices, local(): lax.all_to_all(send_values, 'wide', split_axis=0, concat_axis=0, tiled=True)  7.14 us
    dot_general x1, matrix products, local(): jnp.dot(patch_rows, w_value, preferred_element_type=jnp.float32)  6.52 us
    dot_general x1, matrix products, local(): jnp.dot(patch_rows, w_key, preferred_element_type=jnp.float32)  6.36 us
    dot_general x1, local copies, waits for them, and re-layouts, local(): jnp.dot(patch_rows, w_key, preferred_element_type=jnp.float32)  4.27 us
    all_to_all x1, starting transfers between devices, local(): lax.all_to_all(send_keys, 'wide', split_axis=0, concat_axis=0, tiled=True)  4.24 us
    all_to_all x1, starting transfers between devices, local(): lax.all_to_all(send_values, 'wide', split_axis=0, concat_axis=0, tiled=True)  3.51 us
    reshape x1, local copies, waits for them, and re-layouts, local(): values = values.reshape(images_here, rows_here * kv_cols)  1.44 us
  transfers between devices with their start and end apart: 2, of which 1 were waited for; matrix products, arithmetic and copies ran while one was open for 19% of the time, Pallas kernels for 0%

commit v1 on v0

--- a/solution.py
+++ b/solution.py
@@ -86,7 +86,9 @@
     row_share = batch_here // lax.axis_size("depth")
     numerator, denominator = (
         lax.psum(numerator.astype(jnp.bfloat16), "depth").astype(jnp.float32),
-        lax.psum(denominator.astype(jnp.bfloat16), "depth").astype(jnp.float32),
+        jnp.sum(lax.all_gather(denominator.astype(jnp.bfloat16), "depth"), axis=0).astype(
+            jnp.float32
+        ),
     )
     first_row = lax.axis_index("depth") * row_share
     numerator = lax.dynamic_slice_in_dim(numerator, first_row, row_share, 0)

time: 63.5 us -> 67.3 us (1.060)
  blocking collectives: 19.9 us -> 30.6 us
  waiting for transfers between devices: 7.14 us -> 0.01 us
    all_gather x0 -> x1, blocking collectives: none -> 12.9 us  [local(): lax.all_gather(denominator.astype(jnp.bfloat16), 'depth')]
    all_to_all x1, waiting for transfers between devices: 7.14 us -> 0.01 us  [local(): lax.all_to_all(send_values, 'wide', split_axis=0, concat_axis=0, tiled=True)]
    psum x1, blocking collectives: 19.9 us -> 17.7 us  [local(): lax.psum(numerator.astype(jnp.bfloat16), 'depth').astype(jnp.float32)]
  transfers between devices with their start and end apart: 2 -> 2, of which waited for: 1 -> 0; matrix products, arithmetic and copies ran while one was open for 19% -> 19% of each run, Pallas kernels for 0% -> 0%
where the time goes in v1:
time: 67.3 us; the launch traced here: 66.9 us
  blocking collectives  30.6 us (45%)
  matrix products  16.1 us (24%)
  local copies, waits for them, and re-layouts  8.7 us (13%)
  starting transfers between devices  7.75 us (12%)
  other arithmetic  3.43 us (5%)
    psum x1, blocking collectives, local(): lax.psum(numerator.astype(jnp.bfloat16), 'depth').astype(jnp.float32)  17.7 us
    all_gather x1, blocking collectives, local(): lax.all_gather(denominator.astype(jnp.bfloat16), 'depth')  12.9 us
    dot_general x1, matrix products, local(): jnp.dot(patch_rows, w_value, preferred_element_type=jnp.float32)  6.52 us
    dot_general x1, matrix products, local(): jnp.dot(patch_rows, w_key, preferred_element_type=jnp.float32)  6.36 us
    dot_general x1, local copies, waits for them, and re-layouts, local(): jnp.dot(patch_rows, w_key, preferred_element_type=jnp.float32)  4.27 us
    all_to_all x1, starting transfers between devices, local(): lax.all_to_all(send_keys, 'wide', split_axis=0, concat_axis=0, tiled=True)  4.24 us
    all_to_all x1, starting transfers between devices, local(): lax.all_to_all(send_values, 'wide', split_axis=0, concat_axis=0, tiled=True)  3.51 us
    reshape x1, local copies, waits for them, and re-layouts, local(): values = values.reshape(images_here, rows_here * kv_cols)  1.44 us
  transfers between devices with their start and end apart: 2, of which 0 were waited for; matrix products, arithmetic and copies ran while one was open for 19% of the time, Pallas kernels for 0%

profile of v1, /device:TPU:0, one launch (start us, length us, event | category | flops | bytes accessed | tf_op | source)
XLA Modules:
  0.0 66.9 jit_solution(7649210912033649565)
XLA Ops:
  0.0 4.3 %copy.46 = bf16[256,4096]{1,0:T(8,128)(2,1)} copy(bf16[256,4096]{0,1:T(8,128)(2,1)} %bitcast.51) | data formatting | bytes 4194304 | tf_op jit(solution)/shard_map/dot_general | solution.py:32
  4.3 6.4 %multiply_reduce_fusion = (f32[4,256,2]{1,2,0:T(2,128)S(1)}, f32[4,256,2,128]{1,3,2,0:T(8,128)S(1)}) fusion(bf16[2,128,4096,1]{2,1,0,3:T(8,128)(2,1)} %bitcast.52, bf16[4,256,4096]{2,1,0:T(8,128)(2,1)} %param.10), kind=kOutput, calls=%fused_computation.16 | convolution fusion | flops 2148005888 | bytes 11542528 | tf_op jit(solution)/shard_map/dot_general | solution.py:32
  10.7 0.1 multiply_convert_fusion
  10.8 0.4 copy.30
  11.3 0.2 reshape.209
  11.5 0.1 reshape.190
  11.6 0.6 gather_fusion
  12.3 0.1 reshape.189
  12.3 1.4 %convolution_convert_fusion = bf16[2,2,65536]{2,1,0:T(2,128)(2,1)} fusion(bf16[4,65536,1]{1,0,2:T(4,128)(2,1)S(1)} %reshape.209, s32[4]{0:T(128)S(1)} %iota_add_fusion, s32[2,2]{1,0:T(2,128)S(1)} %reshape.189), kind=kOutput, calls=%fused_computation.2 | convolution fusion | flops 2359312 | bytes 1048608 | tf_op jit(solution)/shard_map/wrj,jx->wrx/dot_general | solution.py:54
  13.7 4.2 %all-to-all-start.1 = ((bf16[2,2,65536]{2,1,0:T(2,128)(2,1)}), bf16[2,2,65536]{2,1,0:T(2,128)(2,1)S(1)}, u32[]{:S(2)}, u32[]{:S(2)}) async-start(bf16[2,2,65536]{2,1,0:T(2,128)(2,1)} %convolution_convert_fusion), calls=%async_computation.1 | async-start | bytes 1048576 | tf_op jit(solution)/shard_map/all_to_all | solution.py:61
  18.0 0.1 multiply_reduce_fusion.1
  18.1 0.1 copy.31
  18.2 0.1 copy.32
  18.3 0.6 gather_fusion.1
  19.0 0.1 compare_convert_fusion
  19.1 0.1 fusion.12
  19.2 6.5 %convolution_convert_fusion.2 = bf16[1024,256]{1,0:T(8,128)(2,1)} fusion(bf16[1024,4096]{1,0:T(8,128)(2,1)} %bitcast.56, bf16[4096,256]{1,0:T(8,128)(2,1)S(1)} %copy-done), kind=kOutput, calls=%fused_computation.6 | convolution fusion | flops 2147745792 | bytes 11010048 | tf_op jit(solution)/shard_map/dot_general | solution.py:40
  25.7 1.4 %reshape.206 = bf16[4,65536,1]{1,0,2:T(4,128)(2,1)S(1)} reshape(bf16[1024,256]{1,0:T(8,128)(2,1)} %convolution_convert_fusion.2) | data formatting | bytes 1048576 | tf_op jit(solution)/shard_map/reshape | solution.py:41
  27.2 1.4 %convolution_convert_fusion.1 = bf16[2,2,65536]{2,1,0:T(2,128)(2,1)} fusion(bf16[4,65536,1]{1,0,2:T(4,128)(2,1)S(1)} %reshape.206, s32[4]{0:T(128)S(1)} %iota_add_fusion, s32[2,2]{1,0:T(2,128)S(1)} %reshape.189), kind=kOutput, calls=%fused_computation.3 | convolution fusion | flops 2359312 | bytes 1048608 | tf_op jit(solution)/shard_map/wrj,jx->wrx/dot_general | solution.py:57
  28.6 3.5 %all-to-all-start = ((bf16[2,2,65536]{2,1,0:T(2,128)(2,1)}), bf16[2,2,65536]{2,1,0:T(2,128)(2,1)S(1)}, u32[]{:S(2)}, u32[]{:S(2)}) async-start(bf16[2,2,65536]{2,1,0:T(2,128)(2,1)} %convolution_convert_fusion.1), calls=%async_computation | async-start | bytes 1048576 | tf_op jit(solution)/shard_map/all_to_all | solution.py:62
  32.1 1.1 %reduce_sum.65 = bf16[2,65536]{1,0:T(2,128)(2,1)S(1)} reduce(bf16[2,2,65536]{2,1,0:T(2,128)(2,1)S(1)} %all-to-all-done.1, bf16[]{:T(256)} %constant.42.clone.1), dimensions={0}, to_apply=%region_2.0 | reduce | flops 131072 | bytes 786434 | tf_op jit(solution)/shard_map/reduce_sum | solution.py:64
  33.2 0.2 reshape.183
  33.4 0.3 fusion.22
  33.7 12.9 %all_gather.4 = bf16[4,16,8]{1,2,0:T(8,128)(2,1)S(1)} all-gather(bf16[1,16,8]{1,2,0:T(8,128)(2,1)S(1)} %bitcast.55), channel_id=1, replica_groups=mesh['wide'=2,'narrow'=4,'depth'=4] {'depth'}, dimensions={0}, use_global_device_ids=true | all-gather | bytes 1280 | tf_op jit(solution)/shard_map/all_gather | solution.py:89
  46.7 0.1 constant_dynamic-slice_fusion
  46.7 0.1 copy.38
  46.8 0.1 broadcast_bitcast_fusion
  46.9 1.1 %reduce_sum.63 = bf16[2,65536]{1,0:T(2,128)(2,1)S(1)} reduce(bf16[2,2,65536]{2,1,0:T(2,128)(2,1)S(1)} %all-to-all-done, bf16[]{:T(256)} %constant.42.clone.1), dimensions={0}, to_apply=%region_0.0 | reduce | flops 131072 | bytes 786434 | tf_op jit(solution)/shard_map/reduce_sum | solution.py:65
  48.1 0.2 reshape.181
  48.3 0.2 fusion.7
  48.5 17.7 %psum.7 = bf16[16,1024]{1,0:T(8,128)(2,1)S(1)} all-reduce(bf16[16,1024]{1,0:T(8,128)(2,1)S(1)} %convert_element_type.81), channel_id=1, replica_groups=mesh['wide'=2,'narrow'=4,'depth'=4] {'depth'}, use_global_device_ids=true, to_apply=%region_4.5 | all-reduce | flops 16384 | bytes 65536 | tf_op jit(solution)/shard_map/psum | solution.py:88
  66.3 0.6 fusion.13
  (32 shorter events, 0.2 us)
Async XLA Ops:
  0.0 19.2 %copy-start = (bf16[4096,256]{1,0:T(8,128)(2,1)S(1)}, bf16[4096,256]{1,0:T(8,128)(2,1)}, u32[]{:S(2)}) copy-start(bf16[4096,256]{1,0:T(8,128)(2,1)} %param.12) | copy-start | bytes 6291460
  4.3 6.4 %copy-start.5 = (f32[128]{0:T(128)S(1)}, f32[128]{0:T(128)}, u32[]{:S(2)}) copy-start(f32[128]{0:T(128)} %param.13) | copy-start | bytes 1540
  10.6 0.8 %copy-start.4 = (s32[2,2]{1,0:T(2,128)S(1)}, s32[2,2]{1,0:T(2,128)}, u32[]{:S(2)}) copy-start(s32[2,2]{1,0:T(2,128)} %param.17) | copy-start | bytes 52
  10.7 1.0 %copy-start.1 = (s32[8]{0:T(128)S(1)}, s32[8]{0:T(128)}, u32[]{:S(2)}) copy-start(s32[8]{0:T(128)} %param.16) | copy-start | bytes 100
  11.3 6.7 %copy-start.3 = (bf16[16,1024]{1,0:T(8,128)(2,1)S(1)}, bf16[16,1024]{1,0:T(8,128)(2,1)}, u32[]{:S(2)}) copy-start(bf16[16,1024]{1,0:T(8,128)(2,1)} %param.15) | copy-start | bytes 98308
  11.3 7.1 %copy-start.2 = (s32[8]{0:T(128)S(1)}, s32[8]{0:T(128)}, u32[]{:S(2)}) copy-start(s32[8]{0:T(128)} %param.19) | copy-start | bytes 100
  11.5 7.6 %copy-start.6 = (f32[128]{0:T(128)S(1)}, f32[128]{0:T(128)}, u32[]{:S(2)}) copy-start(f32[128]{0:T(128)} %param.14) | copy-start | bytes 1540
  13.7 14.9 %all-to-all-start.1 = ((bf16[2,2,65536]{2,1,0:T(2,128)(2,1)}), bf16[2,2,65536]{2,1,0:T(2,128)(2,1)S(1)}, u32[]{:S(2)}, u32[]{:S(2)}) async-start(bf16[2,2,65536]{2,1,0:T(2,128)(2,1)} %convolution_convert_fusion), calls=%async_computation.1 | async-start | bytes 1048576 | tf_op jit(solution)/shard_map/all_to_all | solution.py:61
  19.2 6.5 %copy-start.7 = (s32[16]{0:T(128)S(1)}, s32[16]{0:T(128)}, u32[]{:S(2)}) copy-start(s32[16]{0:T(128)} %param.18) | copy-start | bytes 196
  28.6 18.3 %all-to-all-start = ((bf16[2,2,65536]{2,1,0:T(2,128)(2,1)}), bf16[2,2,65536]{2,1,0:T(2,128)(2,1)S(1)}, u32[]{:S(2)}, u32[]{:S(2)}) async-start(bf16[2,2,65536]{2,1,0:T(2,128)(2,1)} %convolution_convert_fusion.1), calls=%async_computation | async-start | bytes 1048576 | tf_op jit(solution)/shard_map/all_to_all | solution.py:62
